TPU v7x, 32 devices: a whole 2x2x4 slice. The times are simulated.
32 devices in a mesh: left: 8 (over y, x, core), right: 4 (over z).
Axes of the slice: x: 2, y: 2, z: 4, core: 2. Of those that a mesh axis runs over, the one named last changes fastest.
Arguments:
- tracer: float32 [2, 1024, 256, 128], P(None, None, 'left', 'right'), may hold values from -6 to 6
- symbol_x: float32 [1024], replicated, may hold values from 0.3 to 3
- symbol_y: float32 [256], replicated, may hold values from 0.3 to 3
- symbol_z: float32 [128], replicated, may hold values from 0.3 to 3
Outputs:
- modes: float32 [2, 1024, 256, 128], P(None, 'left', 'right')
All inputs are finite; a program needn't handle non-finite values.
Results may differ from a plain program's by a relative error of at most 0.00007.
Values sent between devices are 32-bit elements; how exact they have to be, the bound alone decides.
A program may use at most 256 MiB of HBM per device.

v0:
```python
import functools

import jax
import jax.numpy as jnp
import numpy as np
from jax import lax
from jax.experimental import pallas as pl
from jax.experimental.pallas import tpu as pltpu
from jax.sharding import PartitionSpec as P

MESH = pl.DeviceIdType.MESH
HIGHEST = lax.Precision.HIGHEST
DEPTH = 8
BAND = 16
LANES = 128
SLOTS = 4


def transform_table(count):
    inner = 1 << ((count.bit_length() - 1) // 2)
    outer = count // inner
    column = np.arange(count)

    def angle(row):
        return 2.0 * np.pi / count * (row[:, None] * column[None, :] % count)

    low = angle(np.arange(inner))
    high = angle(np.arange(outer) * inner)
    scale = count ** (-0.5)
    cos_low = jnp.asarray(np.cos(low), jnp.float32)[None]
    sin_low = jnp.asarray(np.sin(low), jnp.float32)[None]
    plus = jnp.asarray((np.cos(high) + np.sin(high)) * scale, jnp.float32)[:, None]
    minus = jnp.asarray((np.cos(high) - np.sin(high)) * scale, jnp.float32)[:, None]
    return (cos_low * plus + sin_low * minus).reshape(count, count)


def landed(ref, sem):
    pltpu.make_async_copy(ref, ref, sem).wait()


def kernel(lefts, rights, data, hx, hy, hz, base, sym_y, out, first, second,
           dbuf, send_a, ybuf, send_b, zbuf, obuf,
           d_sem, sa_sem, ra_sem, y_sem, sb_sem, rb_sem, z_sem, o_sem):
    fields, share_y, share_z, _ = data.shape
    size_y, size_z = hy.shape[0], hz.shape[0]
    share_x = base.shape[0]
    bands = out.shape[1]
    pieces = share_z // DEPTH
    chunks = fields * pieces
    rows = share_y * DEPTH
    flat = DEPTH * BAND
    out_y = bands * BAND
    left, right = lax.axis_index("left"), lax.axis_index("right")

    def load(i):
        source = data.at[i // pieces, :, pl.ds(lax.rem(i, pieces) * DEPTH, DEPTH), :]
        return pltpu.make_async_copy(source, dbuf.at[lax.rem(i, 2)], d_sem.at[lax.rem(i, 2)])

    load(0).start()

    barrier = pltpu.get_barrier_semaphore()
    for k in range(1, lefts):
        pl.semaphore_signal(barrier, inc=1, device_id=(lax.rem(left + k, lefts), right), device_id_type=MESH)
    for k in range(1, rights):
        pl.semaphore_signal(barrier, inc=1, device_id=(left, lax.rem(right + k, rights)), device_id_type=MESH)
    pl.semaphore_wait(barrier, lefts + rights - 2)

    def copy_a(i, to):
        slot = lax.rem(i, SLOTS)
        return pltpu.make_async_remote_copy(
            src_ref=send_a.at[slot, to],
            dst_ref=first.at[i, pl.ds(left * rows, rows)],
            send_sem=sa_sem.at[slot, to],
            recv_sem=ra_sem.at[i, left],
            device_id=(to, right),
            device_id_type=MESH,
        )

    def copy_b(i, to, band):
        spot = right * share_z + lax.rem(i, pieces) * DEPTH
        return pltpu.make_async_remote_copy(
            src_ref=send_b.at[i, to, band],
            dst_ref=second.at[i // pieces, band, pl.ds(spot * BAND, flat)],
            send_sem=sb_sem.at[i, to, band],
            recv_sem=rb_sem.at[i, right, band],
            device_id=(left, to),
            device_id_type=MESH,
        )

    def sent_a(i):
        for k in range(1, lefts):
            copy_a(i, lax.rem(left + k, lefts)).wait_send()

    def x_step(i):
        load(i).wait()

        @pl.when(i + 1 < chunks)
        def _():
            load(i + 1).start()

        @pl.when(i >= SLOTS)
        def _():
            sent_a(i - SLOTS)

        slot = lax.rem(i, SLOTS)

        def tile(j, carry):
            lines = dbuf[lax.rem(i, 2)].reshape(rows, hx.shape[0])
            cols = pl.ds(pl.multiple_of(j * 2 * share_x, 2 * share_x), 2 * share_x)
            got = jnp.dot(lines, hx[:, cols], precision=HIGHEST, preferred_element_type=jnp.float32)
            send_a[slot, 2 * j] = got[:, :share_x]
            send_a[slot, 2 * j + 1] = got[:, share_x:]
            return carry

        lax.fori_loop(0, lefts // 2, tile, 0)
        for k in range(1, lefts):
            copy_a(i, lax.rem(left + k, lefts)).start()
        pltpu.make_async_copy(
            send_a.at[slot, left], first.at[i, pl.ds(left * rows, rows)], ra_sem.at[i, left]
        ).start()

    def y_step(i):
        for k in range(lefts):
            landed(first.at[i, pl.ds(k * rows, rows)], ra_sem.at[i, k])
        fetch = pltpu.make_async_copy(first.at[i], ybuf, y_sem)
        fetch.start()
        fetch.wait()
        for z in range(0, DEPTH, 2):
            pair = jnp.concatenate(
                [ybuf[pl.ds(z, size_y, stride=DEPTH), :], ybuf[pl.ds(z + 1, size_y, stride=DEPTH), :]], axis=1
            )
            got = jnp.dot(hy[...], pair, precision=HIGHEST, preferred_element_type=jnp.float32)
            for to in range(rights):
                for band in range(bands):
                    top = to * out_y + band * BAND
                    for half in range(2):
                        send_b[i, to, band, (z + half) * BAND:(z + half + 1) * BAND, :] = (
                            got[top:top + BAND, half * share_x:(half + 1) * share_x]
                        )
        for band in range(bands):
            for k in range(rights):
                to = jnp.where(right < rights // 2, rights - 1 - k, k)

                @pl.when(to != right)
                def _():
                    copy_b(i, to, band).start()

            spot = right * share_z + lax.rem(i, pieces) * DEPTH
            pltpu.make_async_copy(
                send_b.at[i, right, band],
                second.at[i // pieces, band, pl.ds(spot * BAND, flat)],
                rb_sem.at[i, right, band],
            ).start()

    def step(i, carry):
        @pl.when(i < chunks)
        def _():
            x_step(i)

        @pl.when(i >= 1)
        def _():
            y_step(i - 1)

        return carry

    lax.fori_loop(0, chunks + 1, step, 0)

    def put(n):
        slot = lax.rem(n, 2)
        return pltpu.make_async_copy(obuf.at[slot], out.at[n // bands, lax.rem(n, bands)], o_sem.at[slot])

    def z_step(n, carry):
        field, band = n // bands, lax.rem(n, bands)
        slot = lax.rem(n, 2)

        def arrive(p, carry):
            for k in range(rights):
                spot = k * share_z + p * DEPTH
                landed(second.at[field, band, pl.ds(spot * BAND, flat)], rb_sem.at[field * pieces + p, k, band])
            return carry

        lax.fori_loop(0, pieces, arrive, 0)
        fetch = pltpu.make_async_copy(second.at[field, band], zbuf, z_sem)
        fetch.start()
        fetch.wait()

        @pl.when(n >= 2)
        def _():
            put(n - 2).wait()

        def line(y, carry):
            plane = zbuf[pl.ds(y, size_z, stride=BAND), :].T
            got = jnp.dot(plane, hz[...], precision=HIGHEST, preferred_element_type=jnp.float32)
            got = got * lax.rsqrt(base[...] + sym_y[band * BAND + y])
            for t in range(size_z // LANES):
                obuf[slot, t, pl.ds(y, share_x, stride=BAND), :] = got[:, t * LANES:(t + 1) * LANES]
            return carry

        lax.fori_loop(0, BAND, line, 0, unroll=2)
        put(n).start()
        return carry

    steps = fields * bands
    lax.fori_loop(0, steps, z_step, 0)

    def drain_a(i, carry):
        sent_a(i)
        return carry

    lax.fori_loop(max(chunks - SLOTS, 0), chunks, drain_a, 0)

    def drain_b(i, carry):
        for k in range(1, rights):
            for band in range(bands):
                copy_b(i, lax.rem(right + k, rights), band).wait_send()
        return carry

    lax.fori_loop(0, chunks, drain_b, 0)
    for n in range(max(steps - 2, 0), steps):
        put(n).wait()


def local(lefts, rights, tracer, symbol_x, symbol_y, symbol_z):
    fields, size_x, share_y, share_z = tracer.shape
    size_y, size_z = symbol_y.shape[0], symbol_z.shape[0]
    share_x, out_y = size_x // lefts, size_y // rights
    bands = out_y // BAND
    chunks = fields * (share_z // DEPTH)
    data = jnp.transpose(tracer, (0, 2, 3, 1))
    part_x = lax.dynamic_slice_in_dim(symbol_x, lax.axis_index("left") * share_x, share_x)
    part_y = lax.dynamic_slice_in_dim(symbol_y, lax.axis_index("right") * out_y, out_y)
    base = part_x[:, None] + symbol_z[None, :]
    f32 = jnp.float32
    any_space = pl.BlockSpec(memory_space=pl.ANY)
    vmem = pl.BlockSpec(memory_space=pltpu.VMEM)
    out, _, _ = pl.pallas_call(
        functools.partial(kernel, lefts, rights),
        name="modes",
        out_shape=[
            jax.ShapeDtypeStruct((fields, bands, size_z // LANES, share_x * BAND, LANES), f32),
            jax.ShapeDtypeStruct((chunks, size_y * DEPTH, share_x), f32),
            jax.ShapeDtypeStruct((fields, bands, size_z * BAND, share_x), f32),
        ],
        in_specs=[any_space, vmem, vmem, vmem, vmem, pl.BlockSpec(memory_space=pltpu.SMEM)],
        out_specs=[any_space] * 3,
        scratch_shapes=[
            pltpu.VMEM((2, share_y, DEPTH, size_x), f32),
            pltpu.VMEM((SLOTS, lefts, share_y * DEPTH, share_x), f32),
            pltpu.VMEM((size_y * DEPTH, share_x), f32),
            pltpu.VMEM((chunks, rights, bands, DEPTH * BAND, share_x), f32),
            pltpu.VMEM((size_z * BAND, share_x), f32),
            pltpu.VMEM((2, size_z // LANES, share_x * BAND, LANES), f32),
            pltpu.SemaphoreType.DMA((2,)),
            pltpu.SemaphoreType.DMA((SLOTS, lefts)),
            pltpu.SemaphoreType.DMA((chunks, lefts)),
            pltpu.SemaphoreType.DMA,
            pltpu.SemaphoreType.DMA((chunks, rights, bands)),
            pltpu.SemaphoreType.DMA((chunks, rights, bands)),
            pltpu.SemaphoreType.DMA,
            pltpu.SemaphoreType.DMA((2,)),
        ],
        compiler_params=pltpu.CompilerParams(
            collective_id=0, has_side_effects=True, vmem_limit_bytes=60 * 2**20
        ),
    )(data, transform_table(size_x), transform_table(size_y), transform_table(size_z), base, part_y)
    out = out.reshape(fields, bands, size_z // LANES, share_x, BAND, LANES)
    return jnp.transpose(out, (0, 3, 1, 4, 2, 5)).reshape(fields, share_x, out_y, size_z)


def solution(mesh):
    return jax.shard_map(
        functools.partial(local, mesh.shape["left"], mesh.shape["right"]),
        mesh=mesh,
        in_specs=(P(None, None, "left", "right"), P(), P(), P()),
        out_specs=P(None, "left", "right", None),
        check_vma=False,
    )
```

profile of v0, /device:TPU:1, one launch (start us, length us, event | category | flops | bytes accessed | tf_op | source)
XLA Modules:
  0.0 238.7 jit_solution(13097741636986731579)
XLA Ops:
  0.0 1.3 dynamic_slice.7.sym_y
  1.3 0.8 dynamic_slice.6
  2.0 1.4 broadcast_add_fusion.base
  3.4 1.4 add_bitcast_fusion.hz
  4.8 1.5 multiply_add_fusion.1
  6.3 3.7 %multiply_add_fusion = f32[32,32,1024]{2,1,0:T(8,128)} fusion(f32[32,1024]{1,0:T(8,128)} %constant.46.clone, f32[32,1024]{1,0:T(8,128)} %constant.44.clone, f32[32,1024]{1,0:T(8,128)} %constant.45.clone, f32[32,1024]{1,0:T(8,128)} %constant.43.clone), kind=kLoop, calls=%fused_computation | loop fusion | flops 3145728 | bytes 4718592 | tf_op jit(solution)/shard_map/add | solution.py:34
  10.0 220.6 %modes.1 = (f32[2,4,1,2048,128]{4,3,2,1,0:T(8,128)}, f32[8,2048,128]{2,1,0:T(8,128)}, f32[2,4,2048,128]{3,2,1,0:T(8,128)}) custom-call(f32[2,32,32,1024]{3,2,1,0:T(8,128)} %bitcast.10, f32[1024,1024]{1,0:T(8,128)} %bitcast.9, f32[256,256]{1,0:T(8,128)} %bitcast.12, f32[128,128]{1,0:T(8,128)} %add_bitcast_fusion.hz, f32[128,128]{1,0:T(8,128)} %broadcast_add_fusion.base, ...), custom_call_target="tpu_custom_call" | custom-call | tf_op jit(solution)/shard_map/modes/pallas_call | solution.py:236
  230.6 8.1 %copy.17 = f32[2,128,4,16,1,128]{5,3,2,1,0,4:T(8,128)} copy(f32[2,128,4,16,1,128]{5,3,1,2,0,4:T(8,128)} %bitcast.11) | data formatting | bytes 16777216 | tf_op jit(solution)/shard_map/transpose | solution.py:267
where the time goes:
time: 240 us; the launch traced here: 239 us
  Pallas kernels  221 us (92%)
  local copies, waits for them, and re-layouts  10.1 us (4%)
  other arithmetic  8.01 us (3%)
    pallas_call x1, Pallas kernels, local(): pl.pallas_call(functools.partial(kernel, lefts, rights), name='modes', ou...  221 us
    transpose x1, local copies, waits for them, and re-layouts, local(): jnp.transpose(out, (0, 3, 1, 4, 2, 5))  8.1 us
    add x3, other arithmetic, transform_table(): return (cos_low * plus + sin_low * minus).reshape(count, count)  6.65 us

commit v1 on v0

--- a/solution.py
+++ b/solution.py
@@ -1,4 +1,5 @@
 import functools
+import math
 
 import jax
 import jax.numpy as jnp
@@ -9,11 +10,11 @@
 from jax.sharding import PartitionSpec as P
 
 MESH = pl.DeviceIdType.MESH
-HIGHEST = lax.Precision.HIGHEST
+NEAR_BYTES = 20 * 2**20
 DEPTH = 8
 BAND = 16
 LANES = 128
-SLOTS = 4
+SLOTS = 3
 
 
 def transform_table(count):
@@ -34,15 +35,38 @@
     return (cos_low * plus + sin_low * minus).reshape(count, count)
 
 
+def halves_of(table):
+    upper = lax.reduce_precision(table, 8, 7)
+    return jnp.stack([upper.astype(jnp.bfloat16), (table - upper).astype(jnp.bfloat16)])
+
+
+def small_table(count):
+    rank = np.arange(count)
+    angle = 2.0 * np.pi / count * (rank[:, None] * rank[None, :] % count)
+    table = ((np.cos(angle) + np.sin(angle)) * count ** (-0.5)).astype(np.float32)
+    upper = table.astype(jnp.bfloat16)
+    return jnp.asarray(np.stack([upper, (table - upper.astype(np.float32)).astype(jnp.bfloat16)]))
+
+
+def split(values):
+    upper = values.astype(jnp.bfloat16)
+    return upper, (values - upper.astype(jnp.float32)).astype(jnp.bfloat16)
+
+
+def product(a, b):
+    dot = functools.partial(jnp.dot, preferred_element_type=jnp.float32)
+    return dot(a[0], b[0]) + (dot(a[0], b[1]) + dot(a[1], b[0]))
+
+
 def landed(ref, sem):
     pltpu.make_async_copy(ref, ref, sem).wait()
 
 
-def kernel(lefts, rights, data, hx, hy, hz, base, sym_y, out, first, second,
-           dbuf, send_a, ybuf, send_b, zbuf, obuf,
-           d_sem, sa_sem, ra_sem, y_sem, sb_sem, rb_sem, z_sem, o_sem):
+def kernel(lefts, rights, near, data, hx, hy, hz, base, sym_y, out, *rest):
+    (first, second, dbuf, lines, send_a, send_b, obuf,
+     d_sem, sa_sem, ra_sem, y_sem, sb_sem, rb_sem, z_sem, o_sem, *staging) = rest
     fields, share_y, share_z, _ = data.shape
-    size_y, size_z = hy.shape[0], hz.shape[0]
+    size_y, size_z = hy.shape[1], hz.shape[1]
     share_x = base.shape[0]
     bands = out.shape[1]
     pieces = share_z // DEPTH
@@ -103,11 +127,11 @@
             sent_a(i - SLOTS)
 
         slot = lax.rem(i, SLOTS)
+        lines[0], lines[1] = split(dbuf[lax.rem(i, 2)].reshape(rows, hx.shape[1]))
 
         def tile(j, carry):
-            lines = dbuf[lax.rem(i, 2)].reshape(rows, hx.shape[0])
             cols = pl.ds(pl.multiple_of(j * 2 * share_x, 2 * share_x), 2 * share_x)
-            got = jnp.dot(lines, hx[:, cols], precision=HIGHEST, preferred_element_type=jnp.float32)
+            got = product((lines[0], lines[1]), (hx[0, :, cols], hx[1, :, cols]))
             send_a[slot, 2 * j] = got[:, :share_x]
             send_a[slot, 2 * j + 1] = got[:, share_x:]
             return carry
@@ -122,14 +146,18 @@
     def y_step(i):
         for k in range(lefts):
             landed(first.at[i, pl.ds(k * rows, rows)], ra_sem.at[i, k])
-        fetch = pltpu.make_async_copy(first.at[i], ybuf, y_sem)
-        fetch.start()
-        fetch.wait()
+        if near:
+            block = first.at[i]
+        else:
+            block = staging[0]
+            fetch = pltpu.make_async_copy(first.at[i], block, y_sem)
+            fetch.start()
+            fetch.wait()
         for z in range(0, DEPTH, 2):
             pair = jnp.concatenate(
-                [ybuf[pl.ds(z, size_y, stride=DEPTH), :], ybuf[pl.ds(z + 1, size_y, stride=DEPTH), :]], axis=1
+                [block[pl.ds(z, size_y, stride=DEPTH), :], block[pl.ds(z + 1, size_y, stride=DEPTH), :]], axis=1
             )
-            got = jnp.dot(hy[...], pair, precision=HIGHEST, preferred_element_type=jnp.float32)
+            got = product((hy[0], hy[1]), split(pair))
             for to in range(rights):
                 for band in range(bands):
                     top = to * out_y + band * BAND
@@ -180,18 +208,22 @@
             return carry
 
         lax.fori_loop(0, pieces, arrive, 0)
-        fetch = pltpu.make_async_copy(second.at[field, band], zbuf, z_sem)
-        fetch.start()
-        fetch.wait()
+        if near:
+            block = second.at[field, band]
+        else:
+            block = staging[1]
+            fetch = pltpu.make_async_copy(second.at[field, band], block, z_sem)
+            fetch.start()
+            fetch.wait()
 
         @pl.when(n >= 2)
         def _():
             put(n - 2).wait()
 
         def line(y, carry):
-            plane = zbuf[pl.ds(y, size_z, stride=BAND), :].T
-            got = jnp.dot(plane, hz[...], precision=HIGHEST, preferred_element_type=jnp.float32)
-            got = got * lax.rsqrt(base[...] + sym_y[band * BAND + y])
+            plane = block[pl.ds(y, size_z, stride=BAND), :].T
+            got = product(split(plane), (hz[0], hz[1]))
+            got = got * lax.rsqrt(base[...] + sym_y[right * out_y + band * BAND + y])
             for t in range(size_z // LANES):
                 obuf[slot, t, pl.ds(y, share_x, stride=BAND), :] = got[:, t * LANES:(t + 1) * LANES]
             return carry
@@ -228,27 +260,30 @@
     chunks = fields * (share_z // DEPTH)
     data = jnp.transpose(tracer, (0, 2, 3, 1))
     part_x = lax.dynamic_slice_in_dim(symbol_x, lax.axis_index("left") * share_x, share_x)
-    part_y = lax.dynamic_slice_in_dim(symbol_y, lax.axis_index("right") * out_y, out_y)
     base = part_x[:, None] + symbol_z[None, :]
     f32 = jnp.float32
     any_space = pl.BlockSpec(memory_space=pl.ANY)
     vmem = pl.BlockSpec(memory_space=pltpu.VMEM)
-    out, _, _ = pl.pallas_call(
-        functools.partial(kernel, lefts, rights),
+    landing = [(chunks, size_y * DEPTH, share_x), (fields, bands, size_z * BAND, share_x)]
+    near = 4 * sum(map(math.prod, landing)) <= NEAR_BYTES
+    staging = [] if near else [
+        pltpu.VMEM((size_y * DEPTH, share_x), f32), pltpu.VMEM((size_z * BAND, share_x), f32)
+    ]
+    results = pl.pallas_call(
+        functools.partial(kernel, lefts, rights, near),
         name="modes",
         out_shape=[
             jax.ShapeDtypeStruct((fields, bands, size_z // LANES, share_x * BAND, LANES), f32),
-            jax.ShapeDtypeStruct((chunks, size_y * DEPTH, share_x), f32),
-            jax.ShapeDtypeStruct((fields, bands, size_z * BAND, share_x), f32),
+            *([] if near else [jax.ShapeDtypeStruct(shape, f32) for shape in landing]),
         ],
         in_specs=[any_space, vmem, vmem, vmem, vmem, pl.BlockSpec(memory_space=pltpu.SMEM)],
-        out_specs=[any_space] * 3,
+        out_specs=[any_space] * (1 if near else 3),
         scratch_shapes=[
+            *([pltpu.VMEM(shape, f32) for shape in landing] if near else []),
             pltpu.VMEM((2, share_y, DEPTH, size_x), f32),
+            pltpu.VMEM((2, share_y * DEPTH, size_x), jnp.bfloat16),
             pltpu.VMEM((SLOTS, lefts, share_y * DEPTH, share_x), f32),
-            pltpu.VMEM((size_y * DEPTH, share_x), f32),
             pltpu.VMEM((chunks, rights, bands, DEPTH * BAND, share_x), f32),
-            pltpu.VMEM((size_z * BAND, share_x), f32),
             pltpu.VMEM((2, size_z // LANES, share_x * BAND, LANES), f32),
             pltpu.SemaphoreType.DMA((2,)),
             pltpu.SemaphoreType.DMA((SLOTS, lefts)),
@@ -258,12 +293,13 @@
             pltpu.SemaphoreType.DMA((chunks, rights, bands)),
             pltpu.SemaphoreType.DMA,
             pltpu.SemaphoreType.DMA((2,)),
+            *staging,
         ],
         compiler_params=pltpu.CompilerParams(
             collective_id=0, has_side_effects=True, vmem_limit_bytes=60 * 2**20
         ),
-    )(data, transform_table(size_x), transform_table(size_y), transform_table(size_z), base, part_y)
-    out = out.reshape(fields, bands, size_z // LANES, share_x, BAND, LANES)
+    )(data, halves_of(transform_table(size_x)), small_table(size_y), small_table(size_z), base, symbol_y)
+    out = results[0].reshape(fields, bands, size_z // LANES, share_x, BAND, LANES)
     return jnp.transpose(out, (0, 3, 1, 4, 2, 5)).reshape(fields, share_x, out_y, size_z)
 
 

time: 240 us -> 226 us (0.942)
  Pallas kernels: 221 us -> 210 us
    pallas_call x1, Pallas kernels: 221 us -> 210 us  [local(): pl.pallas_call(functools.partial(kernel, lefts, rights, near), name='mode...]
    add x3 -> x1, other arithmetic: 6.65 us -> 1.71 us  [transform_table(): return (cos_low * plus + sin_low * minus).reshape(count, count)]
where the time goes in v1:
time: 226 us; the launch traced here: 225 us
  Pallas kernels  210 us (93%)
  local copies, waits for them, and re-layouts  8.86 us (4%)
  other arithmetic  6.4 us (3%)
    pallas_call x1, Pallas kernels, local(): pl.pallas_call(functools.partial(kernel, lefts, rights, near), name='mode...  210 us
    transpose x1, local copies, waits for them, and re-layouts, local(): jnp.transpose(out, (0, 3, 1, 4, 2, 5))  8.1 us

profile of v1, /device:TPU:1, one launch (start us, length us, event | category | flops | bytes accessed | tf_op | source)
XLA Modules:
  0.0 225.4 jit_solution(8860441879024706694)
XLA Ops:
  0.0 0.8 dynamic_slice.3
  0.8 1.4 broadcast_add_fusion.base
  2.1 1.7 multiply_add_fusion
  3.9 0.9 reduce-precision_convert_fusion
  4.8 2.4 %pad_maximum_fusion.hx = bf16[2,1024,1024]{2,1,0:T(8,128)(2,1)} fusion(bf16[1,1024,1024]{2,1,0:T(8,128)(2,1)S(1)} %get-tuple-element.6, bf16[1,1024,1024]{2,1,0:T(8,128)(2,1)S(1)} %get-tuple-element.5), kind=kLoop, calls=%fused_computation.3 | loop fusion | flops 2097152 | bytes 8388608 | tf_op jit(solution)/shard_map/stack | solution.py:40
  7.2 210.1 %modes.1 = f32[2,4,1,2048,128]{4,3,2,1,0:T(8,128)} custom-call(f32[2,32,32,1024]{3,2,1,0:T(8,128)} %bitcast.11, bf16[2,1024,1024]{2,1,0:T(8,128)(2,1)} %pad_maximum_fusion.hx, bf16[2,256,256]{2,1,0:T(8,128)(2,1)} %constant.28.clone.hy, bf16[2,128,128]{2,1,0:T(8,128)(2,1)} %constant.29.clone.hz, f32[128,128]{1,0:T(8,128)} %broadcast_add_fusion.base, f32[256]{0:T(256)} %sym_y.1), custom_call_target="tpu_custom_call" | custom-call | tf_op jit(solution)/shard_map/modes/pallas_call | solution.py:272
  217.3 8.1 %copy.11 = f32[2,128,4,16,1,128]{5,3,2,1,0,4:T(8,128)} copy(f32[2,128,4,16,1,128]{5,3,1,2,0,4:T(8,128)} %bitcast.9) | data formatting | bytes 16777216 | tf_op jit(solution)/shard_map/transpose | solution.py:303
